TPU v7x, 32 devices: a whole 2x2x4 slice. The times are simulated.
32 devices in a mesh: fsdp: 8 (over z, core), tp: 4 (over y, x).
Axes of the slice: x: 2, y: 2, z: 4, core: 2. Of those that a mesh axis runs over, the one named last changes fastest.
Arguments:
- hidden_in: bfloat16 [512, 4096], P('fsdp'), may hold values from -3 to 3
- queries: bfloat16 [2, 512, 8192], P(None, ('fsdp', 'tp')), may hold values from -170 to 170
- key_cache: bfloat16 [512, 256, 512], P(('fsdp', 'tp')), may hold values from -6 to 6
- value_cache: bfloat16 [512, 256, 512], P(('fsdp', 'tp')), may hold values from -6 to 6
- new_keys: bfloat16 [2, 512, 512], P(None, ('fsdp', 'tp')), may hold values from -6 to 6
- new_values: bfloat16 [2, 512, 512], P(None, ('fsdp', 'tp')), may hold values from -6 to 6
- lengths: int32 [512], P(('fsdp', 'tp')), may hold values from 2 to 256
- routes: int32 [2, 512, 8], P(None, 'fsdp'), may hold values from 0 to 127, all different within a row; in each aligned block of 64 rows (0 to 63, 64 to 127, ..., all dimensions but the last counted through in order) at most 8 rows name the same one
- route_weights: float32 [2, 512, 8], P(None, 'fsdp'), may hold values from 0.05 to 1
- norm_gain: float32 [4096], replicated, may hold values from 0.1 to 1.9
- gate_master: float32 [8, 1536, 4096], P(None, ('fsdp', 'tp')), may hold values from -0.09375 to 0.09375
- up_master: float32 [8, 1536, 4096], P(None, ('fsdp', 'tp')), may hold values from -0.09375 to 0.09375
- down_master: float32 [8, 1536, 4096], P(None, ('fsdp', 'tp')), may hold values from -0.3125 to 0.3125
- out_proj: bfloat16 [8192, 4096], P('tp'), may hold values from -0.0625 to 0.0625
Outputs:
- hidden_out: bfloat16 [512, 4096], P('fsdp', 'tp')
- scale_log2: float32 [3, 8, 12, 32], replicated
Inputs may be any that keep to these rules, and one draw needn't show every extreme that they name: `routes`: within one step and one index of fsdp (aligned blocks of 64 rows), no expert is named by more than 8 rows.
All inputs are finite; a program needn't handle non-finite values.
Results may differ from a plain program's by a relative error of at most 0.0095.
Values may be sent and summed in bfloat16 or wider, within the bound.
No kernel may reach another device: no remote copies, remote signals or barrier semaphores. Data moves between devices by JAX's collectives and lax.ppermute only.
A program may use at most 384 MiB of HBM per device.

v0:
```python
import jax
import jax.numpy as jnp
from jax import lax
from jax.sharding import PartitionSpec as P

D = 4096
FF = 1536
QH = 64
KVH = 4
HD = 128
BLOCK = 128
WIN = 8
CAP = 8
neg_fill = -1e30
epsilon = 1e-06
fp_limit = 448.0
grid_floor = 2.0 ** (-10)
least_exponent = -6.0


def grid_round(values):
    magnitude = jnp.abs(values)
    exponent = jnp.maximum(jnp.floor(jnp.log2(jnp.maximum(magnitude, grid_floor))), least_exponent)
    spacing = jnp.exp2(exponent - 3.0)
    return jnp.sign(values) * jnp.floor(magnitude / spacing + 0.5) * spacing


def row_scales(scales, owner_map):
    return jnp.einsum(
        "sb,xwbc->xwsc", owner_map.astype(jnp.float32), scales, precision=lax.Precision.HIGHEST
    )


def owner_blocks(owner_rows):
    return (owner_rows // BLOCK)[:, None] == jnp.arange(FF // BLOCK, dtype=jnp.int32)[None, :]


def dequantize(shard_piece, shard_rows, tp_count, tp_pos, scales):
    count = shard_piece.shape[2]
    gathered_index = jnp.arange(count, dtype=jnp.int32)
    owner_rows = (
        gathered_index // shard_rows * tp_count + tp_pos
    ) * shard_rows + gathered_index % shard_rows
    factors = row_scales(scales, owner_blocks(owner_rows))
    tiles = shard_piece.astype(jnp.float32).reshape(3, WIN, count, D // BLOCK, BLOCK)
    return (tiles * factors[..., None]).astype(jnp.bfloat16).reshape(3, WIN, count, D)


def attention_rows(queries_now, cache_keys, cache_values, fresh_keys, fresh_values, lengths):
    row_count = queries_now.shape[0]
    positions = cache_keys.shape[1]
    group = QH // KVH
    score_scale = HD ** (-0.5)
    fresh_count = fresh_keys.shape[0]
    query_heads = queries_now.reshape(row_count, KVH, group, HD)
    key_heads = cache_keys.reshape(row_count, positions, KVH, HD)
    value_heads = cache_values.reshape(row_count, positions, KVH, HD)
    fresh_key_heads = fresh_keys.reshape(fresh_count, row_count, KVH, HD)
    fresh_value_heads = fresh_values.reshape(fresh_count, row_count, KVH, HD)
    cached_scores = (
        jnp.einsum("rkgd,rpkd->rkgp", query_heads, key_heads, preferred_element_type=jnp.float32)
        * score_scale
    )
    fresh_scores = (
        jnp.einsum(
            "rkgd,srkd->rkgs", query_heads, fresh_key_heads, preferred_element_type=jnp.float32
        )
        * score_scale
    )
    alive_mask = (jnp.arange(positions, dtype=jnp.int32)[None, :] < lengths[:, None])[
        :, None, None, :
    ]
    peak_score = jnp.maximum(
        jnp.max(jnp.where(alive_mask, cached_scores, neg_fill), axis=-1),
        jnp.max(fresh_scores, axis=-1),
    )
    cached_weights = jnp.where(alive_mask, jnp.exp(cached_scores - peak_score[..., None]), 0.0)
    fresh_weights = jnp.exp(fresh_scores - peak_score[..., None])
    weight_sum = jnp.sum(cached_weights, axis=-1) + jnp.sum(fresh_weights, axis=-1)
    cached_probs = (cached_weights / weight_sum[..., None]).astype(jnp.bfloat16)
    fresh_probs = (fresh_weights / weight_sum[..., None]).astype(jnp.bfloat16)
    output = jnp.einsum(
        "rkgp,rpkd->rkgd", cached_probs, value_heads, preferred_element_type=jnp.float32
    )
    output = output + jnp.einsum(
        "rkgs,srkd->rkgd", fresh_probs, fresh_value_heads, preferred_element_type=jnp.float32
    )
    return output.astype(jnp.bfloat16).reshape(row_count, QH * HD)


def routing_tables(routes, route_weights, capacity):
    weight_sum = jnp.sum(route_weights, axis=1)
    experts = jnp.arange(WIN, dtype=jnp.int32)
    matches = routes[None, :, :] == experts[:, None, None]
    chosen = jnp.any(matches, axis=2)
    gate_share = (
        jnp.sum(jnp.where(matches, route_weights[None, :, :], 0.0), axis=2) / weight_sum[None, :]
    )
    slot_index = jnp.cumsum(chosen.astype(jnp.int32), axis=1) - 1
    places = jnp.arange(capacity, dtype=jnp.int32)
    picked = (slot_index[:, None, :] == places[None, :, None]) & chosen[:, None, :]
    return (picked.astype(jnp.bfloat16), picked.astype(jnp.float32) * gate_share[:, None, :])


def expert_rows(selected, gate_rows, up_rows, down_rows):
    gate_act = jnp.einsum("ecd,ehd->ech", selected, gate_rows, preferred_element_type=jnp.float32)
    up_act = jnp.einsum("ecd,ehd->ech", selected, up_rows, preferred_element_type=jnp.float32)
    product = (jax.nn.silu(gate_act) * up_act).astype(jnp.bfloat16)
    return jnp.einsum("ech,ehd->ecd", product, down_rows, preferred_element_type=jnp.float32)


def local_experts(selected, weighted, restored):
    outputs = expert_rows(selected, restored[0], restored[1], restored[2])
    return jnp.einsum("ecr,ecd->rd", weighted, outputs, precision=lax.Precision.HIGHEST)


def local(
    hidden_in,
    queries,
    key_cache,
    value_cache,
    new_keys,
    new_values,
    lengths,
    routes,
    route_weights,
    norm_gain,
    gate_master,
    up_master,
    down_master,
    out_proj,
):
    tp_count = lax.axis_size("tp")
    fsdp_pos = lax.axis_index("fsdp")
    tp_pos = lax.axis_index("tp")
    shard_rows = gate_master.shape[1]
    masters = jnp.stack([gate_master, up_master, down_master])
    owned_rows = (fsdp_pos * tp_count + tp_pos) * shard_rows + jnp.arange(
        shard_rows, dtype=jnp.int32
    )
    owner_map = owner_blocks(owned_rows)
    magnitude = jnp.max(jnp.abs(masters).reshape(3, WIN, shard_rows, D // BLOCK, BLOCK), axis=4)
    partial_max = jnp.max(
        jnp.where(owner_map[None, None, :, :, None], magnitude[:, :, :, None, :], 0.0), axis=2
    )
    block_max = lax.pmax(partial_max, ("fsdp", "tp"))
    scales = (block_max + epsilon) / fp_limit
    scale_log2 = jnp.log2(scales)
    local_factors = row_scales(scales, owner_map)
    tiles = masters.reshape(3, WIN, shard_rows, D // BLOCK, BLOCK)
    quantized = (
        grid_round(tiles / local_factors[..., None])
        .astype(jnp.bfloat16)
        .reshape(3, WIN, shard_rows, D)
    )
    gathered = lax.all_gather(quantized, "fsdp", axis=2, tiled=True)
    restored = dequantize(gathered, shard_rows, tp_count, tp_pos, scales)
    share_cols = D // tp_count
    own_start = tp_pos * share_cols
    current = lax.dynamic_slice_in_dim(hidden_in, own_start, share_cols, 1)
    for step_index in range(2):
        heads_local = attention_rows(
            queries[step_index],
            key_cache,
            value_cache,
            new_keys[: step_index + 1],
            new_values[: step_index + 1],
            lengths,
        )
        regrouped = lax.all_to_all(heads_local, "tp", split_axis=1, concat_axis=0, tiled=True)
        projected = jnp.dot(regrouped, out_proj, preferred_element_type=jnp.float32)
        mixed = (
            current.astype(jnp.float32)
            + lax.psum_scatter(projected, "tp", scatter_dimension=1, tiled=True)
        ).astype(jnp.bfloat16)
        values = mixed.astype(jnp.float32)
        squares = lax.psum(jnp.sum(values * values, axis=1), "tp")
        inverse = lax.rsqrt(squares / D + epsilon)
        own_gain = lax.dynamic_slice_in_dim(norm_gain, own_start, share_cols, 0)
        normed_share = (values * inverse[:, None] * own_gain[None, :]).astype(jnp.bfloat16)
        normed = lax.all_gather(normed_share, "tp", axis=1, tiled=True)
        picked, weighted = routing_tables(routes[step_index], route_weights[step_index], CAP)
        selected = jnp.einsum(
            "ecr,rd->ecd", picked, normed, preferred_element_type=jnp.float32
        ).astype(jnp.bfloat16)
        partial_value = local_experts(selected, weighted, restored)
        current = (
            mixed.astype(jnp.float32)
            + lax.psum_scatter(partial_value, "tp", scatter_dimension=1, tiled=True)
        ).astype(jnp.bfloat16)
    return (current, scale_log2)


def solution(mesh):
    in_specs = (
        P("fsdp", None),
        P(None, ("fsdp", "tp"), None),
        P(("fsdp", "tp"), None, None),
        P(("fsdp", "tp"), None, None),
        P(None, ("fsdp", "tp"), None),
        P(None, ("fsdp", "tp"), None),
        P(("fsdp", "tp")),
        P(None, "fsdp", None),
        P(None, "fsdp", None),
        P(),
        P(None, ("fsdp", "tp"), None),
        P(None, ("fsdp", "tp"), None),
        P(None, ("fsdp", "tp"), None),
        P("tp", None),
    )
    out_specs = (P("fsdp", "tp"), P())
    return jax.shard_map(local, mesh=mesh, in_specs=in_specs, out_specs=out_specs, check_vma=False)
```

profile of v0, /device:TPU:0, one launch (start us, length us, event | category | flops | bytes accessed | tf_op | source)
XLA Modules:
  0.0 1244.2 jit_solution(15809943041866484468)
XLA Ops:
  8.0 1.1 slice_bitcast_fusion.1
  10.9 3.5 select_reduce_fusion.2
  14.5 0.9 copy-done.5
  15.4 3.5 fusion.37
  19.0 0.9 slice_convert_fusion
  19.9 4.0 fusion.28
  23.9 1.0 all_to_all.28
  24.9 0.9 copy.67
  25.8 5.2 all-to-all-start
  31.0 4.2 copy.90
  35.2 4.1 copy.89
  39.3 1.3 copy.88
  40.6 5.2 fusion
  46.1 1.3 select_reduce_fusion
  47.4 44.0 %pmax.7 = f32[3,8,12,32]{3,2,1,0:T(8,128)S(1)} all-reduce(f32[3,8,12,32]{3,2,1,0:T(8,128)S(1)} %select_reduce_fusion), channel_id=1, replica_groups=mesh['fsdp'=8,'tp'=4] {'fsdp','tp'}, use_global_device_ids=true, to_apply=%region_11.12 | all-reduce | flops 9216 | bytes 73728 | tf_op jit(solution)/shard_map/pmax | solution.py:146
  92.1 7.1 div.130
  99.2 20.5 %div.131 = f32[3,8,48,4096]{3,2,1,0:T(8,128)} reshape(f32[3,8,48,32,128]{4,3,2,1,0:T(8,128)} %div.130) | data formatting | bytes 37748736 | tf_op jit(solution)/shard_map/div | solution.py:152
  119.7 9.8 fusion.125
  129.6 22.2 %multiply_convert_fusion.1 = bf16[3,8,48,4096]{3,2,1,0:T(8,128)(2,1)} fusion(f32[3,8,48,4096]{3,2,1,0:T(8,128)} %div.131, f32[1,8,48,4096]{3,2,1,0:T(8,128)} %bitcast.146, f32[1,8,48,4096]{3,2,1,0:T(8,128)} %bitcast.148, f32[1,8,48,4096]{3,2,1,0:T(8,128)} %bitcast.149), kind=kLoop, calls=%fused_computation.4 | loop fusion | flops 80216064 | bytes 47185920 | tf_op jit(solution)/shard_map/convert_element_type | solution.py:153
  153.0 3.0 fusion.25
  156.1 0.9 copy.77
  156.9 3.4 all-to-all-start.1
  161.2 3.9 copy.71
  166.6 1.2 slice_reduce_fusion
  168.4 13.6 %fusion.127 = f32[64,4096]{1,0:T(8,128)} fusion(bf16[64,2048]{1,0:T(8,128)(2,1)S(1)} %bitcast.154, bf16[2048,4096]{1,0:T(8,128)(2,1)} %param.27), kind=kOutput, calls=%fused_computation.184 | convolution fusion | flops 1073741824 | bytes 18087936 | tf_op jit(solution)/shard_map/dot_general | solution.py:171
  182.2 1.2 fusion.49
  183.4 10.4 psum.14
  193.9 10.0 all_gather.9
  203.9 1.1 convolution_convert_fusion.1
  205.0 579.8 %all-gather.2.cloned.1.call-done = bf16[3,8,384,4096]{3,2,1,0:T(8,128)(2,1)} async-done(((bf16[3,8,48,4096]{3,2,1,0:T(8,128)(2,1)}), bf16[3,8,384,4096]{3,2,1,0:T(8,128)(2,1)}) %all-gather.2.cloned.1.call-update) | async-done | bytes 75497488 | tf_op jit(solution)/shard_map/all_gather | solution.py:156
  784.7 74.7 %copy.91 = f32[1152,8,32,128]{3,2,1,0:T(8,128)} copy(bf16[1152,8,32,128]{3,1,2,0:T(8,128)(2,1)} %bitcast.100) | data formatting | bytes 226492416
  859.4 73.6 %multiply_convert_fusion = bf16[3,8,384,32,128]{4,3,2,1,0:T(8,128)(2,1)} fusion(f32[3,8,384,32,128]{4,3,2,1,0:T(8,128)} %bitcast.53, f32[3,8,384,32]{3,2,1,0:T(8,128)} %copy.71), kind=kLoop, calls=%fused_computation | loop fusion | flops 75497472 | bytes 227672064 | tf_op jit(solution)/shard_map/convert_element_type | solution.py:46
  933.1 50.2 %fusion.122 = (bf16[1,8,384,32,128]{4,3,2,1,0:T(8,128)(2,1)}, bf16[1,8,384,32,128]{4,3,2,1,0:T(8,128)(2,1)}, bf16[1,8,384,32,128]{4,3,2,1,0:T(8,128)(2,1)}) fusion(bf16[3,8,384,32,128]{4,3,2,1,0:T(8,128)(2,1)} %multiply_convert_fusion), kind=kLoop, calls=%fused_computation.179 | loop fusion | bytes 150994944 | tf_op jit(solution)/shard_map/slice | solution.py:113
  983.3 37.3 %squeeze.16 = bf16[8,384,4096]{2,1,0:T(8,128)(2,1)} reshape(bf16[1,8,384,32,128]{4,3,2,1,0:T(8,128)(2,1)} %get-tuple-element.19) | data formatting | bytes 50331648 | tf_op jit(solution)/shard_map/squeeze | solution.py:113
  1020.6 37.4 %squeeze.7 = bf16[8,384,4096]{2,1,0:T(8,128)(2,1)} reshape(bf16[1,8,384,32,128]{4,3,2,1,0:T(8,128)(2,1)} %get-tuple-element.20) | data formatting | bytes 50331648 | tf_op jit(solution)/shard_map/squeeze | solution.py:113
  1058.0 37.3 %squeeze.6 = bf16[8,384,4096]{2,1,0:T(8,128)(2,1)} reshape(bf16[1,8,384,32,128]{4,3,2,1,0:T(8,128)(2,1)} %get-tuple-element.18) | data formatting | bytes 50331648 | tf_op jit(solution)/shard_map/squeeze | solution.py:113
  1095.3 11.5 fusion.126
  1106.9 18.2 %fusion.34 = f32[8,8,4096]{2,1,0:T(8,128)S(1)} fusion(bf16[8,384,4096]{2,1,0:T(8,128)(2,1)} %squeeze.16, bf16[8,8,4096]{2,1,0:T(8,128)(2,1)S(1)} %copy-done, bf16[8,384,4096]{2,1,0:T(8,128)(2,1)} %squeeze.7, f32[8,8,384]{2,1,0:T(8,128)S(1)} %fusion.126), kind=kOutput, calls=%fused_computation.35 | convolution fusion | flops 402800640 | bytes 52002816 | tf_op jit(solution)/shard_map/ech,ehd->ecd/dot_general | solution.py:109
  1125.1 2.6 convolution_bitcast_fusion.1
  1128.2 26.0 %reduce-scatter.7.cloned.1.call-done = f32[64,1024]{1,0:T(8,128)} async-done(((f32[64,4096]{1,0:T(8,128)}), f32[64,1024]{1,0:T(8,128)}) %reduce-scatter.7.cloned.1.call-update) | async-done | bytes 262160 | tf_op jit(solution)/shard_map/reduce_scatter | solution.py:189
  1154.1 1.2 fusion.53
  1155.3 8.9 psum.15
  1164.4 10.2 all_gather.11
  1174.9 11.5 fusion.128
  1186.4 18.2 %fusion.32 = f32[8,8,4096]{2,1,0:T(8,128)S(1)} fusion(bf16[8,384,4096]{2,1,0:T(8,128)(2,1)} %squeeze.16, bf16[8,8,4096]{2,1,0:T(8,128)(2,1)S(1)} %convolution_convert_fusion, bf16[8,384,4096]{2,1,0:T(8,128)(2,1)} %squeeze.7, f32[8,8,384]{2,1,0:T(8,128)S(1)} %fusion.128), kind=kOutput, calls=%fused_computation.32 | convolution fusion | flops 402800640 | bytes 52002816 | tf_op jit(solution)/shard_map/ech,ehd->ecd/dot_general | solution.py:109
  1204.6 2.6 convolution_bitcast_fusion
  1208.0 27.3 %reduce-scatter.11.cloned.1.call-done = f32[64,1024]{1,0:T(8,128)} async-done(((f32[64,4096]{1,0:T(8,128)}), f32[64,1024]{1,0:T(8,128)}) %reduce-scatter.11.cloned.1.call-update) | async-done | bytes 262160 | tf_op jit(solution)/shard_map/reduce_scatter | solution.py:189
  1235.3 1.6 fusion.56
  (110 shorter events, 9.0 us)
Async XLA Ops:
  9.1 5.3 copy-start.6
  14.4 1.0 copy-start.5
  18.9 20.3 %slice-start = ((s8[6291456]{0:T(1024)(128)(4,1)}), s8[2097152]{0:T(1024)(128)(4,1)S(1)}, s32[]{:S(2)}) async-start(s8[6291456]{0:T(1024)(128)(4,1)} %bitcast.150), calls=%async_computation.11 | async-start | bytes 4194304
  25.8 93.9 %all-to-all-start = ((bf16[16,4,2048]{2,0,1:T(8,128)(2,1)}), bf16[16,4,2048]{2,0,1:T(8,128)(2,1)S(1)}, u32[]{:S(2)}, u32[]{:S(2)}) async-start(bf16[16,4,2048]{2,0,1:T(8,128)(2,1)} %copy.67), calls=%async_computation | async-start | bytes 524288 | tf_op jit(solution)/shard_map/all_to_all | solution.py:170
  31.0 151.2 %reduce-scatter.5.cloned.1.call-start = ((), (), s32[]{:S(2)}) async-start(), calls=%async_computation.6 | async-start | bytes 1310720 | tf_op jit(solution)/shard_map/reduce_scatter | solution.py:174
  31.0 8.3 slice-start.1
  91.3 69.1 %copy-start.1 = (f32[3,8,12,32]{3,2,1,0:T(8,128)}, f32[3,8,12,32]{3,2,1,0:T(8,128)S(1)}, u32[]{:S(2)}) copy-start(f32[3,8,12,32]{3,2,1,0:T(8,128)S(1)} %pmax.7) | copy-start | bytes 110596
  129.5 655.3 %all-gather.2.cloned.1.call-start = ((), (), s32[]{:S(2)}) async-start(), calls=%async_computation.7 | async-start | bytes 84934656 | tf_op jit(solution)/shard_map/all_gather | solution.py:156
  129.5 22.3 %copy-start.9 = (bf16[2,16,512]{2,1,0:T(8,128)(2,1)S(1)}, bf16[2,16,512]{2,1,0:T(8,128)(2,1)}, u32[]{:S(2)}) copy-start(bf16[2,16,512]{2,1,0:T(8,128)(2,1)} %param.18) | copy-start | bytes 98308
  129.5 22.3 %copy-start.8 = (bf16[2,16,512]{2,1,0:T(8,128)(2,1)S(1)}, bf16[2,16,512]{2,1,0:T(8,128)(2,1)}, u32[]{:S(2)}) copy-start(bf16[2,16,512]{2,1,0:T(8,128)(2,1)} %param.19) | copy-start | bytes 98308
  129.5 22.3 %copy-start.7 = (bf16[2,8,64,128]{3,2,1,0:T(8,128)(2,1)S(1)}, bf16[2,8,64,128]{3,2,1,0:T(8,128)(2,1)}, u32[]{:S(2)}) copy-start(bf16[2,8,64,128]{3,2,1,0:T(8,128)(2,1)} %copy-done.6) | copy-start | bytes 786436
  151.7 13.3 %copy-start.19 = (s32[2,64,8]{1,2,0:T(8,128)S(1)}, s32[2,64,8]{1,2,0:T(8,128)}, u32[]{:S(2)}) copy-start(s32[2,64,8]{1,2,0:T(8,128)} %param.21) | copy-start | bytes 12292
  151.7 14.9 %copy-start.20 = (f32[2,64,8]{1,2,0:T(8,128)S(1)}, f32[2,64,8]{1,2,0:T(8,128)}, u32[]{:S(2)}) copy-start(f32[2,64,8]{1,2,0:T(8,128)} %param.22) | copy-start | bytes 12292
  156.9 11.5 all-to-all-start.1
  160.4 967.8 %reduce-scatter.9.cloned.1.call-start = ((), (), s32[]{:S(2)}) async-start(), calls=%async_computation.9 | async-start | bytes 1310720 | tf_op jit(solution)/shard_map/reduce_scatter | solution.py:174
  165.7 16.5 %copy-start.16 = (pred[8,64]{1,0:T(8,128)(4,1)}, pred[8,64]{1,0:T(8,128)(4,1)S(1)}, u32[]{:S(2)}) copy-start(pred[8,64]{1,0:T(8,128)(4,1)S(1)} %fusion.82) | copy-start | bytes 1540
  166.6 692.8 %copy-start.10 = (f32[1024]{0:T(1024)}, f32[1024]{0:T(1024)S(1)}, u32[]{:S(2)}) copy-start(f32[1024]{0:T(1024)S(1)} %dynamic_slice.8) | copy-start | bytes 12292
  167.8 691.6 %copy-start.12 = (s32[8,64]{1,0:T(8,128)}, s32[8,64]{1,0:T(8,128)S(1)}, u32[]{:S(2)}) copy-start(s32[8,64]{1,0:T(8,128)S(1)} %broadcast_add_fusion.1) | copy-start | bytes 6148
  182.1 972.0 %reduce-scatter.7.cloned.1.call-start = ((), (), s32[]{:S(2)}) async-start(), calls=%async_computation.8 | async-start | bytes 1310720 | tf_op jit(solution)/shard_map/reduce_scatter | solution.py:189
  183.4 676.0 %copy-start.3 = (bf16[64,1024]{1,0:T(8,128)(2,1)}, bf16[64,1024]{1,0:T(8,128)(2,1)S(1)}, u32[]{:S(2)}) copy-start(bf16[64,1024]{1,0:T(8,128)(2,1)S(1)} %get-tuple-element.17) | copy-start | bytes 393220
  1058.0 37.3 %copy-start = (bf16[8,8,4096]{2,1,0:T(8,128)(2,1)S(1)}, bf16[8,8,4096]{2,1,0:T(8,128)(2,1)}, u32[]{:S(2)}) copy-start(bf16[8,8,4096]{2,1,0:T(8,128)(2,1)} %convolution_convert_fusion.1) | copy-start | bytes 1572868
  1106.8 18.3 %copy-start.13 = (s32[8,64]{1,0:T(8,128)S(1)}, s32[8,64]{1,0:T(8,128)}, u32[]{:S(2)}) copy-start(s32[8,64]{1,0:T(8,128)} %copy-done.12) | copy-start | bytes 6148
  1106.8 18.3 %copy-start.15 = (f32[8,64]{1,0:T(8,128)S(1)}, f32[8,64]{1,0:T(8,128)}, u32[]{:S(2)}) copy-start(f32[8,64]{1,0:T(8,128)} %broadcast_divide_fusion.1) | copy-start | bytes 6148
  1106.8 18.3 %copy-start.17 = (pred[8,64]{1,0:T(8,128)(4,1)S(1)}, pred[8,64]{1,0:T(8,128)(4,1)}, u32[]{:S(2)}) copy-start(pred[8,64]{1,0:T(8,128)(4,1)} %copy-done.16) | copy-start | bytes 1540
  1106.9 20.9 %copy-start.14 = (s32[64,8]{0,1:T(8,128)S(1)}, s32[64,8]{0,1:T(8,128)}, u32[]{:S(2)}) copy-start(s32[64,8]{0,1:T(8,128)} %get-tuple-element.26) | copy-start | bytes 6148
  1106.9 21.2 %copy-start.18 = (f32[64,8]{0,1:T(8,128)S(1)}, f32[64,8]{0,1:T(8,128)}, u32[]{:S(2)}) copy-start(f32[64,8]{0,1:T(8,128)} %get-tuple-element.25) | copy-start | bytes 6148
  1106.9 21.2 %copy-start.21 = (f32[64]{0:T(128)S(1)}, f32[64]{0:T(128)}, u32[]{:S(2)}) copy-start(f32[64]{0:T(128)} %get-tuple-element.10) | copy-start | bytes 772
  1106.9 47.2 %copy-start.4 = (bf16[64,1024]{1,0:T(8,128)(2,1)S(1)}, bf16[64,1024]{1,0:T(8,128)(2,1)}, u32[]{:S(2)}) copy-start(bf16[64,1024]{1,0:T(8,128)(2,1)} %copy-done.3) | copy-start | bytes 393220
  1106.9 57.3 %copy-start.11 = (f32[1024]{0:T(1024)S(1)}, f32[1024]{0:T(1024)}, u32[]{:S(2)}) copy-start(f32[1024]{0:T(1024)} %copy-done.10) | copy-start | bytes 12292
  1127.8 107.5 %reduce-scatter.11.cloned.1.call-start = ((), (), s32[]{:S(2)}) async-start(), calls=%async_computation.10 | async-start | bytes 1310720 | tf_op jit(solution)/shard_map/reduce_scatter | solution.py:189
  1186.4 20.8 %copy-start.2 = (f32[3,8,12,32]{3,2,1,0:T(8,128)S(1)}, f32[3,8,12,32]{3,2,1,0:T(8,128)}, u32[]{:S(2)}) copy-start(f32[3,8,12,32]{3,2,1,0:T(8,128)} %copy-done.1) | copy-start | bytes 110596
Sparse Core Ops, SparseCore 0:
  129.6 26.9 reduce-scatter.4
  182.2 29.3 reduce-scatter.8
  1127.9 26.2 reduce-scatter.6
  1207.3 27.9 reduce-scatter.10
Sparse Core Ops, SparseCore 1:
  151.9 632.8 all-gather.1
where the time goes:
time: 1260 us; the launch traced here: 1240 us
  waiting for transfers between devices  633 us (50%)
  local copies, waits for them, and re-layouts  286 us (23%)
  other arithmetic  111 us (9%)
  matrix products  105 us (8%)
  blocking collectives  83.5 us (7%)
  between operations  16 us (1%)
    all_gather x1, waiting for transfers between devices, local(): gathered = lax.all_gather(quantized, 'fsdp', axis=2, tiled=True)  580 us
    squeeze x3, local copies, waits for them, and re-layouts, local_experts(): outputs = expert_rows(selected, restored[0], restored[1], restored[2])  112 us
    unnamed x56, local copies, waits for them, and re-layouts  87.2 us
    convert_element_type x1, other arithmetic, dequantize(): (tiles * factors[..., None]).astype(jnp.bfloat16).reshape(3, WIN, count, D)  73.6 us
    reduce_scatter x2, waiting for transfers between devices, local(): lax.psum_scatter(partial_value, 'tp', scatter_dimension=1, tiled=True)  53.3 us
    slice x1, local copies, waits for them, and re-layouts, local_experts(): outputs = expert_rows(selected, restored[0], restored[1], restored[2])  50.2 us
    pmax x1, blocking collectives, local(): block_max = lax.pmax(partial_max, ('fsdp', 'tp'))  44 us
    dot_general x2, matrix products, expert_rows(): jnp.einsum('ech,ehd->ecd', product, down_rows, preferred_element_type=jnp...  36.4 us
  transfers between devices with their start and end apart: 7, of which 3 were waited for; matrix products, arithmetic and copies ran while one was open for 35% of the time, Pallas kernels for 0%

commit v1 on v0

--- a/solution.py
+++ b/solution.py
@@ -153,7 +153,12 @@
         .astype(jnp.bfloat16)
         .reshape(3, WIN, shard_rows, D)
     )
-    gathered = lax.all_gather(quantized, "fsdp", axis=2, tiled=True)
+    ring = [quantized]
+    for hop in range(7):
+        ring.append(lax.ppermute(ring[-1], "fsdp", [(dev, (dev + 1) % 8) for dev in range(8)]))
+    gathered = jnp.roll(
+        jnp.concatenate(ring[::-1], axis=2), (lax.axis_index("fsdp") + 1) * ring[0].shape[2], axis=2
+    )
     restored = dequantize(gathered, shard_rows, tp_count, tp_pos, scales)
     share_cols = D // tp_count
     own_start = tp_pos * share_cols

time: 1260 us -> 1610 us (1.28)
  local copies, waits for them, and re-layouts: 286 us -> 445 us
  other arithmetic: 111 us -> 229 us
  waiting for transfers between devices: 633 us -> 719 us
    ppermute x0 -> x7, waiting for transfers between devices: none -> 651 us  [local(): lax.ppermute(ring[-1], 'fsdp', [(dev, (dev + 1) % 8) for dev in range(8)])]
    all_gather x1 -> x0, waiting for transfers between devices: 580 us -> none  [local(): gathered = lax.all_gather(quantized, 'fsdp', axis=2, tiled=True)]
    unnamed x56 -> x78, local copies, waits for them, and re-layouts: 87.2 us -> 249 us
    reshape x0 -> x1, other arithmetic: none -> 77.8 us  [dequantize(): shard_piece.astype(jnp.float32).reshape(3, WIN, count, D // BLOCK, BLOCK)]
    unnamed x1 -> x2, other arithmetic: 0.01 us -> 22.1 us
    concatenate x0 -> x1, other arithmetic: none -> 21.9 us  [local(): jnp.roll(jnp.concatenate(ring[::-1], axis=2), (lax.axis_index('fsdp') + 1...]
  transfers between devices with their start and end apart: 7 -> 13, of which waited for: 3 -> 10; matrix products, arithmetic and copies ran while one was open for 35% -> 41% of each run, Pallas kernels for 0% -> 0%
where the time goes in v1:
time: 1610 us; the launch traced here: 1600 us
  waiting for transfers between devices  719 us (45%)
  local copies, waits for them, and re-layouts  445 us (28%)
  other arithmetic  229 us (14%)
  matrix products  101 us (6%)
  blocking collectives  84.4 us (5%)
    ppermute x7, waiting for transfers between devices, local(): lax.ppermute(ring[-1], 'fsdp', [(dev, (dev + 1) % 8) for dev in range(8)])  651 us
    unnamed x78, local copies, waits for them, and re-layouts  249 us
    squeeze x3, local copies, waits for them, and re-layouts, local_experts(): outputs = expert_rows(selected, restored[0], restored[1], restored[2])  112 us
    reshape x1, other arithmetic, dequantize(): shard_piece.astype(jnp.float32).reshape(3, WIN, count, D // BLOCK, BLOCK)  77.8 us
    convert_element_type x1, other arithmetic, dequantize(): (tiles * factors[..., None]).astype(jnp.bfloat16).reshape(3, WIN, count, D)  73.6 us
    reduce_scatter x2, waiting for transfers between devices, local(): lax.psum_scatter(partial_value, 'tp', scatter_dimension=1, tiled=True)  52.2 us
    slice x1, local copies, waits for them, and re-layouts, local_experts(): outputs = expert_rows(selected, restored[0], restored[1], restored[2])  50.3 us
    pmax x1, blocking collectives, local(): block_max = lax.pmax(partial_max, ('fsdp', 'tp'))  44.7 us
  transfers between devices with their start and end apart: 13, of which 10 were waited for; matrix products, arithmetic and copies ran while one was open for 41% of the time, Pallas kernels for 0%

profile of v1, /device:TPU:0, one launch (start us, length us, event | category | flops | bytes accessed | tf_op | source)
XLA Modules:
  0.0 1601.3 jit_solution(5705239455727097145)
XLA Ops:
  16.9 5.2 fusion
  23.6 44.7 %pmax.7 = f32[3,8,12,32]{3,2,1,0:T(8,128)S(1)} all-reduce(f32[3,8,12,32]{3,2,1,0:T(8,128)S(1)} %select_reduce_fusion), channel_id=1, replica_groups=mesh['fsdp'=8,'tp'=4] {'fsdp','tp'}, use_global_device_ids=true, to_apply=%region_11.12 | all-reduce | flops 9216 | bytes 73728 | tf_op jit(solution)/shard_map/pmax | solution.py:146
  69.1 7.1 div.130
  76.2 20.4 %div.131 = f32[3,8,48,4096]{3,2,1,0:T(8,128)} reshape(f32[3,8,48,32,128]{4,3,2,1,0:T(8,128)} %div.130) | data formatting | bytes 37748736 | tf_op jit(solution)/shard_map/div | solution.py:152
  96.6 19.6 %multiply_convert_fusion.1 = bf16[3,8,48,4096]{3,2,1,0:T(8,128)(2,1)S(1)} fusion(f32[3,8,48,4096]{3,2,1,0:T(8,128)} %div.131, f32[1,8,48,4096]{3,2,1,0:T(8,128)} %bitcast.141, f32[1,8,48,4096]{3,2,1,0:T(8,128)} %bitcast.148, f32[1,8,48,4096]{3,2,1,0:T(8,128)} %bitcast.152), kind=kLoop, calls=%fused_computation.5 | loop fusion | flops 80216064 | bytes 47185920 | tf_op jit(solution)/shard_map/convert_element_type | solution.py:153
  116.3 105.9 %collective-permute-done = bf16[3,8,48,4096]{3,2,1,0:T(8,128)(2,1)S(1)} collective-permute-done((bf16[3,8,48,4096]{3,2,1,0:T(8,128)(2,1)S(1)}, bf16[3,8,48,4096]{3,2,1,0:T(8,128)(2,1)S(1)}, u32[]{:S(2)}, u32[]{:S(2)}) %collective-permute-start) | collective-permute-done | bytes 9437216 | tf_op jit(solution)/shard_map/ppermute | solution.py:158
  225.9 105.9 %collective-permute-done.1 = bf16[3,8,48,4096]{3,2,1,0:T(8,128)(2,1)S(1)} collective-permute-done((bf16[3,8,48,4096]{3,2,1,0:T(8,128)(2,1)S(1)}, bf16[3,8,48,4096]{3,2,1,0:T(8,128)(2,1)S(1)}, u32[]{:S(2)}, u32[]{:S(2)}) %collective-permute-start.1) | collective-permute-done | bytes 9437216 | tf_op jit(solution)/shard_map/ppermute | solution.py:158
  335.4 105.9 %collective-permute-done.2 = bf16[3,8,48,4096]{3,2,1,0:T(8,128)(2,1)S(1)} collective-permute-done((bf16[3,8,48,4096]{3,2,1,0:T(8,128)(2,1)S(1)}, bf16[3,8,48,4096]{3,2,1,0:T(8,128)(2,1)S(1)}, u32[]{:S(2)}, u32[]{:S(2)}) %collective-permute-start.2) | collective-permute-done | bytes 9437216 | tf_op jit(solution)/shard_map/ppermute | solution.py:158
  444.9 105.9 %collective-permute-done.3 = bf16[3,8,48,4096]{3,2,1,0:T(8,128)(2,1)S(1)} collective-permute-done((bf16[3,8,48,4096]{3,2,1,0:T(8,128)(2,1)S(1)}, bf16[3,8,48,4096]{3,2,1,0:T(8,128)(2,1)S(1)}, u32[]{:S(2)}, u32[]{:S(2)}) %collective-permute-start.3) | collective-permute-done | bytes 9437216 | tf_op jit(solution)/shard_map/ppermute | solution.py:158
  554.4 105.9 %collective-permute-done.4 = bf16[3,8,48,4096]{3,2,1,0:T(8,128)(2,1)S(1)} collective-permute-done((bf16[3,8,48,4096]{3,2,1,0:T(8,128)(2,1)S(1)}, bf16[3,8,48,4096]{3,2,1,0:T(8,128)(2,1)S(1)}, u32[]{:S(2)}, u32[]{:S(2)}) %collective-permute-start.4) | collective-permute-done | bytes 9437216 | tf_op jit(solution)/shard_map/ppermute | solution.py:158
  664.0 106.0 %collective-permute-done.5 = bf16[3,8,48,4096]{3,2,1,0:T(8,128)(2,1)} collective-permute-done((bf16[3,8,48,4096]{3,2,1,0:T(8,128)(2,1)S(1)}, bf16[3,8,48,4096]{3,2,1,0:T(8,128)(2,1)}, u32[]{:S(2)}, u32[]{:S(2)}) %collective-permute-start.5) | collective-permute-done | bytes 9437216 | tf_op jit(solution)/shard_map/ppermute | solution.py:158
  798.4 9.7 fusion.125
  812.2 10.0 fusion.127
  822.2 15.0 reduce-scatter.5.cloned.1.call-done
  838.3 8.9 psum.14
  847.3 11.9 all_gather.6
  860.3 16.0 collective-permute-done.6
  876.3 8.6 constant_dynamic-update-slice_fusion.15
  884.9 8.6 constant_dynamic-update-slice_fusion.14
  893.4 8.7 constant_dynamic-update-slice_fusion.13
  902.1 8.6 constant_dynamic-update-slice_fusion.12
  910.7 8.6 constant_dynamic-update-slice_fusion.11
  919.3 8.6 constant_dynamic-update-slice_fusion.10
  927.9 8.6 constant_dynamic-update-slice_fusion.9
  936.5 22.1 %constant_dynamic-update-slice_fusion.8 = bf16[3,8,768,4096]{3,2,1,0:T(8,128)(2,1)} fusion(bf16[3,8,768,4096]{3,2,1,0:T(8,128)(2,1)} %constant_dynamic-update-slice_fusion.9, f32[3,8,48,4096]{3,2,1,0:T(8,128)} %div.131, f32[1,8,48,4096]{3,2,1,0:T(8,128)} %bitcast.142, f32[1,8,48,4096]{3,2,1,0:T(8,128)} %bitcast.149, f32[1,8,48,4096]{3,2,1,0:T(8,128)} %bitcast.153), kind=kLoop, calls=%fused_computation.104 | loop fusion | flops 80216064 | bytes 47185920
  958.6 8.7 constant_dynamic-update-slice_fusion.7
  967.3 8.7 constant_dynamic-update-slice_fusion.6
  976.0 8.7 constant_dynamic-update-slice_fusion.5
  984.6 8.6 constant_dynamic-update-slice_fusion.4
  993.3 8.8 constant_dynamic-update-slice_fusion.3
  1002.0 8.7 constant_dynamic-update-slice_fusion.2
  1010.7 8.6 constant_dynamic-update-slice_fusion.1
  1019.3 21.9 %constant_dynamic-update-slice_fusion = bf16[3,8,768,4096]{3,2,1,0:T(8,128)(2,1)} fusion(bf16[3,8,768,4096]{3,2,1,0:T(8,128)(2,1)} %constant_dynamic-update-slice_fusion.1, f32[3,8,48,4096]{3,2,1,0:T(8,128)} %div.131, f32[1,8,48,4096]{3,2,1,0:T(8,128)} %bitcast.143, f32[1,8,48,4096]{3,2,1,0:T(8,128)} %bitcast.150, f32[1,8,48,4096]{3,2,1,0:T(8,128)} %bitcast.154), kind=kLoop, calls=%fused_computation.96 | loop fusion | flops 80216064 | bytes 47185920 | tf_op jit(solution)/shard_map/jit(_roll_dynamic)/concatenate | solution.py:159
  1041.2 77.8 %dynamic-slice_convert_fusion = f32[3,8,384,4096]{3,2,1,0:T(8,128)} fusion(bf16[3,8,768,4096]{3,2,1,0:T(8,128)(2,1)} %constant_dynamic-update-slice_fusion, s32[]{:T(128)S(6)} %select_n.84), kind=kLoop, calls=%fused_computation.1 | loop fusion | flops 37748736 | bytes 226492416 | tf_op jit(solution)/shard_map/reshape | solution.py:45
  1119.0 98.8 %copy.91 = f32[1152,8,32,128]{3,2,1,0:T(8,128)} copy(f32[1152,8,32,128]{3,1,2,0:T(8,128)} %bitcast.51) | data formatting | bytes 301989888
  1217.8 73.6 %multiply_convert_fusion = bf16[3,8,384,32,128]{4,3,2,1,0:T(8,128)(2,1)} fusion(f32[3,8,384,32,128]{4,3,2,1,0:T(8,128)} %bitcast.53, f32[3,8,384,32]{3,2,1,0:T(8,128)} %copy.71), kind=kLoop, calls=%fused_computation | loop fusion | flops 75497472 | bytes 227672064 | tf_op jit(solution)/shard_map/convert_element_type | solution.py:46
  1291.5 50.3 %fusion.122 = (bf16[1,8,384,32,128]{4,3,2,1,0:T(8,128)(2,1)}, bf16[1,8,384,32,128]{4,3,2,1,0:T(8,128)(2,1)}, bf16[1,8,384,32,128]{4,3,2,1,0:T(8,128)(2,1)}) fusion(bf16[3,8,384,32,128]{4,3,2,1,0:T(8,128)(2,1)} %multiply_convert_fusion), kind=kLoop, calls=%fused_computation.196 | loop fusion | bytes 150994944 | tf_op jit(solution)/shard_map/slice | solution.py:113
  1341.7 37.3 %squeeze.6 = bf16[8,384,4096]{2,1,0:T(8,128)(2,1)} reshape(bf16[1,8,384,32,128]{4,3,2,1,0:T(8,128)(2,1)} %get-tuple-element.18) | data formatting | bytes 50331648 | tf_op jit(solution)/shard_map/squeeze | solution.py:113
  1379.1 37.4 %squeeze.16 = bf16[8,384,4096]{2,1,0:T(8,128)(2,1)} reshape(bf16[1,8,384,32,128]{4,3,2,1,0:T(8,128)(2,1)} %get-tuple-element.19) | data formatting | bytes 50331648 | tf_op jit(solution)/shard_map/squeeze | solution.py:113
  1416.4 37.3 %squeeze.7 = bf16[8,384,4096]{2,1,0:T(8,128)(2,1)} reshape(bf16[1,8,384,32,128]{4,3,2,1,0:T(8,128)(2,1)} %get-tuple-element.20) | data formatting | bytes 50331648 | tf_op jit(solution)/shard_map/squeeze | solution.py:113
  1453.8 11.5 fusion.126
  1465.3 18.2 %fusion.34 = f32[8,8,4096]{2,1,0:T(8,128)S(1)} fusion(bf16[8,384,4096]{2,1,0:T(8,128)(2,1)} %squeeze.16, bf16[8,8,4096]{2,1,0:T(8,128)(2,1)S(1)} %copy-done.5, bf16[8,384,4096]{2,1,0:T(8,128)(2,1)} %squeeze.7, f32[8,8,384]{2,1,0:T(8,128)S(1)} %fusion.126), kind=kOutput, calls=%fused_computation.36 | convolution fusion | flops 402800640 | bytes 52002816 | tf_op jit(solution)/shard_map/ech,ehd->ecd/dot_general | solution.py:109
  1486.6 24.9 %reduce-scatter.7.cloned.1.call-done = f32[64,1024]{1,0:T(8,128)} async-done(((f32[64,4096]{1,0:T(8,128)}), f32[64,1024]{1,0:T(8,128)}) %reduce-scatter.7.cloned.1.call-update) | async-done | bytes 262160 | tf_op jit(solution)/shard_map/reduce_scatter | solution.py:194
  1512.7 8.9 psum.15
  1521.8 10.0 all_gather.7
  1532.1 11.8 fusion.128
  1543.8 18.2 %fusion.32 = f32[8,8,4096]{2,1,0:T(8,128)S(1)} fusion(bf16[8,384,4096]{2,1,0:T(8,128)(2,1)} %squeeze.16, bf16[8,8,4096]{2,1,0:T(8,128)(2,1)S(1)} %convolution_convert_fusion, bf16[8,384,4096]{2,1,0:T(8,128)(2,1)} %squeeze.7, f32[8,8,384]{2,1,0:T(8,128)S(1)} %fusion.128), kind=kOutput, calls=%fused_computation.33 | convolution fusion | flops 402800640 | bytes 52002816 | tf_op jit(solution)/shard_map/ech,ehd->ecd/dot_general | solution.py:109
  1565.4 27.3 %reduce-scatter.11.cloned.1.call-done = f32[64,1024]{1,0:T(8,128)} async-done(((f32[64,4096]{1,0:T(8,128)}), f32[64,1024]{1,0:T(8,128)}) %reduce-scatter.11.cloned.1.call-update) | async-done | bytes 262160 | tf_op jit(solution)/shard_map/reduce_scatter | solution.py:194
  (147 shorter events, 74.2 us)
Async XLA Ops:
  7.2 8.4 slice-start
  7.2 8.3 slice-start.1
  68.3 721.3 %copy-start.6 = (f32[3,8,12,32]{3,2,1,0:T(8,128)}, f32[3,8,12,32]{3,2,1,0:T(8,128)S(1)}, u32[]{:S(2)}) copy-start(f32[3,8,12,32]{3,2,1,0:T(8,128)S(1)} %pmax.7) | copy-start | bytes 110596
  96.6 673.5 %copy-start.10 = (bf16[2,16,8192]{2,1,0:T(8,128)(2,1)S(1)}, bf16[2,16,8192]{2,1,0:T(8,128)(2,1)}, u32[]{:S(2)}) copy-start(bf16[2,16,8192]{2,1,0:T(8,128)(2,1)} %param.15) | copy-start | bytes 1572868
  96.6 673.5 %slice-start.2 = ((bf16[2,16,512]{2,1,0:T(8,128)(2,1)}), bf16[1,16,512]{2,1,0:T(8,128)(2,1)S(1)}, s32[]{:S(2)}) async-start(bf16[2,16,512]{2,1,0:T(8,128)(2,1)} %param.18), calls=%async_computation.12 | async-start | bytes 32768 | tf_op jit(solution)/shard_map/slice | solution.py:171
  96.6 673.6 %copy-start.11 = (bf16[2,16,512]{2,1,0:T(8,128)(2,1)S(1)}, bf16[2,16,512]{2,1,0:T(8,128)(2,1)}, u32[]{:S(2)}) copy-start(bf16[2,16,512]{2,1,0:T(8,128)(2,1)} %param.19) | copy-start | bytes 98308
  96.6 673.7 %copy-start.25 = (s32[16]{0:T(128)S(1)}, s32[16]{0:T(128)}, u32[]{:S(2)}) copy-start(s32[16]{0:T(128)} %param.20) | copy-start | bytes 196
  116.3 669.2 %copy-start.12 = (bf16[2,16,512]{2,1,0:T(8,128)(2,1)S(1)}, bf16[2,16,512]{2,1,0:T(8,128)(2,1)}, u32[]{:S(2)}) copy-start(bf16[2,16,512]{2,1,0:T(8,128)(2,1)} %param.18) | copy-start | bytes 98308
  116.3 106.0 %collective-permute-start = (bf16[3,8,48,4096]{3,2,1,0:T(8,128)(2,1)S(1)}, bf16[3,8,48,4096]{3,2,1,0:T(8,128)(2,1)S(1)}, u32[]{:S(2)}, u32[]{:S(2)}) collective-permute-start(bf16[3,8,48,4096]{3,2,1,0:T(8,128)(2,1)S(1)} %multiply_convert_fusion.1), channel_id=1, source_target_pairs={{0,4},{4,8},{8,12},{12,16},{16,20},{20,24},{24,28},{28,0},{1,5},{5... | collective-permute-start | bytes 28311560 | tf_op jit(solution)/shard_map/ppermute | solution.py:158
  222.2 3.6 copy-start
  225.9 105.9 %collective-permute-start.1 = (bf16[3,8,48,4096]{3,2,1,0:T(8,128)(2,1)S(1)}, bf16[3,8,48,4096]{3,2,1,0:T(8,128)(2,1)S(1)}, u32[]{:S(2)}, u32[]{:S(2)}) collective-permute-start(bf16[3,8,48,4096]{3,2,1,0:T(8,128)(2,1)S(1)} %collective-permute-done), channel_id=1, source_target_pairs={{0,4},{4,8},{8,12},{12,16},{16,20},{20,24},{24,28},{28,0},{1,5},{5... | collective-permute-start | bytes 28311560 | tf_op jit(solution)/shard_map/ppermute | solution.py:158
  331.8 3.6 copy-start.1
  335.4 105.9 %collective-permute-start.2 = (bf16[3,8,48,4096]{3,2,1,0:T(8,128)(2,1)S(1)}, bf16[3,8,48,4096]{3,2,1,0:T(8,128)(2,1)S(1)}, u32[]{:S(2)}, u32[]{:S(2)}) collective-permute-start(bf16[3,8,48,4096]{3,2,1,0:T(8,128)(2,1)S(1)} %collective-permute-done.1), channel_id=1, source_target_pairs={{0,4},{4,8},{8,12},{12,16},{16,20},{20,24},{24,28},{28,0},{1,5},{5... | collective-permute-start | bytes 28311560 | tf_op jit(solution)/shard_map/ppermute | solution.py:158
  441.3 3.6 copy-start.2
  444.9 105.9 %collective-permute-start.3 = (bf16[3,8,48,4096]{3,2,1,0:T(8,128)(2,1)S(1)}, bf16[3,8,48,4096]{3,2,1,0:T(8,128)(2,1)S(1)}, u32[]{:S(2)}, u32[]{:S(2)}) collective-permute-start(bf16[3,8,48,4096]{3,2,1,0:T(8,128)(2,1)S(1)} %collective-permute-done.2), channel_id=1, source_target_pairs={{0,4},{4,8},{8,12},{12,16},{16,20},{20,24},{24,28},{28,0},{1,5},{5... | collective-permute-start | bytes 28311560 | tf_op jit(solution)/shard_map/ppermute | solution.py:158
  550.8 3.6 copy-start.3
  554.4 105.9 %collective-permute-start.4 = (bf16[3,8,48,4096]{3,2,1,0:T(8,128)(2,1)S(1)}, bf16[3,8,48,4096]{3,2,1,0:T(8,128)(2,1)S(1)}, u32[]{:S(2)}, u32[]{:S(2)}) collective-permute-start(bf16[3,8,48,4096]{3,2,1,0:T(8,128)(2,1)S(1)} %collective-permute-done.3), channel_id=1, source_target_pairs={{0,4},{4,8},{8,12},{12,16},{16,20},{20,24},{24,28},{28,0},{1,5},{5... | collective-permute-start | bytes 28311560 | tf_op jit(solution)/shard_map/ppermute | solution.py:158
  660.3 3.7 copy-start.4
  664.0 106.0 %collective-permute-start.5 = (bf16[3,8,48,4096]{3,2,1,0:T(8,128)(2,1)S(1)}, bf16[3,8,48,4096]{3,2,1,0:T(8,128)(2,1)}, u32[]{:S(2)}, u32[]{:S(2)}) collective-permute-start(bf16[3,8,48,4096]{3,2,1,0:T(8,128)(2,1)S(1)} %collective-permute-done.4), channel_id=1, source_target_pairs={{0,4},{4,8},{8,12},{12,16},{16,20},{20,24},{24,28},{28,0},{1,5},{5... | collective-permute-start | bytes 28311560 | tf_op jit(solution)/shard_map/ppermute | solution.py:158
  770.0 106.2 %collective-permute-start.6 = (bf16[3,8,48,4096]{3,2,1,0:T(8,128)(2,1)}, bf16[3,8,48,4096]{3,2,1,0:T(8,128)(2,1)}, u32[]{:S(2)}, u32[]{:S(2)}) collective-permute-start(bf16[3,8,48,4096]{3,2,1,0:T(8,128)(2,1)} %collective-permute-done.5), channel_id=1, source_target_pairs={{0,4},{4,8},{8,12},{12,16},{16,20},{20,24},{24,28},{28,0},{1,5},{5... | collective-permute-start | bytes 28311560 | tf_op jit(solution)/shard_map/ppermute | solution.py:158
  781.6 12.7 all-to-all-start
  789.7 18.6 %copy-start.22 = (s32[2,64,8]{1,2,0:T(8,128)S(1)}, s32[2,64,8]{1,2,0:T(8,128)}, u32[]{:S(2)}) copy-start(s32[2,64,8]{1,2,0:T(8,128)} %param.21) | copy-start | bytes 12292
  789.7 20.1 %copy-start.23 = (f32[2,64,8]{1,2,0:T(8,128)S(1)}, f32[2,64,8]{1,2,0:T(8,128)}, u32[]{:S(2)}) copy-start(f32[2,64,8]{1,2,0:T(8,128)} %param.22) | copy-start | bytes 12292
  794.3 17.9 %all-to-all-start.1 = ((bf16[16,4,2048]{2,0,1:T(8,128)(2,1)}), bf16[16,4,2048]{2,0,1:T(8,128)(2,1)S(1)}, u32[]{:S(2)}, u32[]{:S(2)}) async-start(bf16[16,4,2048]{2,0,1:T(8,128)(2,1)} %copy.77), calls=%async_computation.3 | async-start | bytes 524288 | tf_op jit(solution)/shard_map/all_to_all | solution.py:175
  798.4 38.7 %reduce-scatter.5.cloned.1.call-start = ((), (), s32[]{:S(2)}) async-start(), calls=%async_computation.6 | async-start | bytes 1310720 | tf_op jit(solution)/shard_map/reduce_scatter | solution.py:179
  808.2 678.4 %reduce-scatter.9.cloned.1.call-start = ((), (), s32[]{:S(2)}) async-start(), calls=%async_computation.8 | async-start | bytes 1310720 | tf_op jit(solution)/shard_map/reduce_scatter | solution.py:179
  808.9 76.0 %copy-start.19 = (pred[8,64]{1,0:T(8,128)(4,1)}, pred[8,64]{1,0:T(8,128)(4,1)S(1)}, u32[]{:S(2)}) copy-start(pred[8,64]{1,0:T(8,128)(4,1)S(1)} %fusion.82) | copy-start | bytes 1540
  809.8 75.0 %copy-start.13 = (f32[1024]{0:T(1024)}, f32[1024]{0:T(1024)S(1)}, u32[]{:S(2)}) copy-start(f32[1024]{0:T(1024)S(1)} %dynamic_slice.12) | copy-start | bytes 12292
  811.0 0.6 copy-start.15
  822.1 689.4 %reduce-scatter.7.cloned.1.call-start = ((), (), s32[]{:S(2)}) async-start(), calls=%async_computation.7 | async-start | bytes 1310720 | tf_op jit(solution)/shard_map/reduce_scatter | solution.py:194
  838.3 55.1 %copy-start.8 = (bf16[64,1024]{1,0:T(8,128)(2,1)}, bf16[64,1024]{1,0:T(8,128)(2,1)S(1)}, u32[]{:S(2)}) copy-start(bf16[64,1024]{1,0:T(8,128)(2,1)S(1)} %get-tuple-element.17) | copy-start | bytes 393220
  1416.4 37.3 %copy-start.5 = (bf16[8,8,4096]{2,1,0:T(8,128)(2,1)S(1)}, bf16[8,8,4096]{2,1,0:T(8,128)(2,1)}, u32[]{:S(2)}) copy-start(bf16[8,8,4096]{2,1,0:T(8,128)(2,1)} %convolution_convert_fusion.1) | copy-start | bytes 1572868
  1465.3 18.3 %copy-start.16 = (s32[8,64]{1,0:T(8,128)S(1)}, s32[8,64]{1,0:T(8,128)}, u32[]{:S(2)}) copy-start(s32[8,64]{1,0:T(8,128)} %copy-done.15) | copy-start | bytes 6148
  1465.3 18.3 %copy-start.18 = (f32[8,64]{1,0:T(8,128)S(1)}, f32[8,64]{1,0:T(8,128)}, u32[]{:S(2)}) copy-start(f32[8,64]{1,0:T(8,128)} %broadcast_divide_fusion.1) | copy-start | bytes 6148
  1465.3 18.3 %copy-start.20 = (pred[8,64]{1,0:T(8,128)(4,1)S(1)}, pred[8,64]{1,0:T(8,128)(4,1)}, u32[]{:S(2)}) copy-start(pred[8,64]{1,0:T(8,128)(4,1)} %copy-done.19) | copy-start | bytes 1540
  1465.3 21.0 %copy-start.17 = (s32[64,8]{0,1:T(8,128)S(1)}, s32[64,8]{0,1:T(8,128)}, u32[]{:S(2)}) copy-start(s32[64,8]{0,1:T(8,128)} %get-tuple-element.26) | copy-start | bytes 6148
  1465.3 21.2 %copy-start.21 = (f32[64,8]{0,1:T(8,128)S(1)}, f32[64,8]{0,1:T(8,128)}, u32[]{:S(2)}) copy-start(f32[64,8]{0,1:T(8,128)} %get-tuple-element.25) | copy-start | bytes 6148
  1465.3 21.2 %copy-start.24 = (f32[64]{0:T(128)S(1)}, f32[64]{0:T(128)}, u32[]{:S(2)}) copy-start(f32[64]{0:T(128)} %get-tuple-element.10) | copy-start | bytes 772
  1465.3 46.2 %copy-start.9 = (bf16[64,1024]{1,0:T(8,128)(2,1)S(1)}, bf16[64,1024]{1,0:T(8,128)(2,1)}, u32[]{:S(2)}) copy-start(bf16[64,1024]{1,0:T(8,128)(2,1)} %copy-done.8) | copy-start | bytes 393220
  1465.3 56.4 %copy-start.14 = (f32[1024]{0:T(1024)S(1)}, f32[1024]{0:T(1024)}, u32[]{:S(2)}) copy-start(f32[1024]{0:T(1024)} %copy-done.13) | copy-start | bytes 12292
  1486.2 106.5 %reduce-scatter.11.cloned.1.call-start = ((), (), s32[]{:S(2)}) async-start(), calls=%async_computation.9 | async-start | bytes 1310720 | tf_op jit(solution)/shard_map/reduce_scatter | solution.py:194
  1543.8 20.8 %copy-start.7 = (f32[3,8,12,32]{3,2,1,0:T(8,128)S(1)}, f32[3,8,12,32]{3,2,1,0:T(8,128)}, u32[]{:S(2)}) copy-start(f32[3,8,12,32]{3,2,1,0:T(8,128)} %copy-done.6) | copy-start | bytes 110596
Sparse Core Ops, SparseCore 0:
  808.3 28.7 reduce-scatter.4
  840.0 29.9 reduce-scatter.8
  1486.3 25.1 reduce-scatter.6
  1564.7 27.8 reduce-scatter.10
